TPU v7x, 32 devices: a whole 2x2x4 slice. The times are simulated.
32 devices in a mesh: groups: 2 (over y), gx: 4 (over z), gy: 4 (over x, core).
Axes of the slice: x: 2, y: 2, z: 4, core: 2. Of those that a mesh axis runs over, the one named last changes fastest.
Arguments:
- thermal_deviation: float32 [32, 256, 512], P('groups', 'gy', 'gx'), parts along dimension 0, may hold values from -6 to 6
- brine_content: float32 [32, 256, 512], P('groups', 'gy', 'gx'), parts along dimension 0, may hold values from 0.2 to 2.4
- current_components: float32 [4, 16, 256, 512], P('groups', None, 'gy', 'gx'), parts along dimension 0, may hold values from -4 to 4
- sea_indicator: int32 [256, 512], P('gy', 'gx'), may hold values from 0 to 1, as said below
- flooded_layer_number: int32 [256, 512], P('gy', 'gx'), may hold values from 1 to 16
- footprint_square_metres: float32 [256, 512], P('gy', 'gx'), may hold values from 0.5 to 5
- rainfall_input: float32 [256, 512], P('gy', 'gx'), may hold values from -2 to 3.5
- seam_partner_index: int32 [512], P('gx'), may hold values from 0 to 511, as said below
Outputs:
- temperature_next: float32 [32, 256, 512], P('groups', 'gy', 'gx'), parts along dimension 0
- salinity_next: float32 [32, 256, 512], P('groups', 'gy', 'gx'), parts along dimension 0
There are 2 independent parts, one for each index of `groups`. A program takes and returns all parts, laid end to end along the dimension named above; an argument that names none is the same for every part. Nothing has to cross between parts.
Inputs may be any that keep to these rules, and one draw needn't show every extreme that they name: `sea_indicator`: at least one column is ocean. seam_partner_index[x] = (s - x) mod 512 for one s of each draw with s mod 128 = 127; the map is its own inverse and has no fixed point.
All inputs are finite; a program needn't handle non-finite values.
Results may differ from a plain program's by a relative error of at most 0.00002.
Values sent between devices are 32-bit elements; how exact they have to be, the bound alone decides.
A program may use at most 64 MiB of HBM per device.

v0:
```python
import jax
import jax.numpy as jnp
from jax import lax
from jax.sharding import PartitionSpec as P

time_step = 0.25
diffusivity = 0.5
vertical_mixing = 0.3
top_thickness = 0.5


def with_halo(cells, sides, width, closed):
    for axis, dim in sides:
        count = lax.axis_size(axis)
        ends = count if closed else count - 1
        head = lax.slice_in_dim(cells, 0, width, axis=dim)
        tail = lax.slice_in_dim(cells, cells.shape[dim] - width, cells.shape[dim], axis=dim)
        cells = jnp.concatenate(
            [
                lax.ppermute(tail, axis, [(i, (i + 1) % count) for i in range(ends)]),
                cells,
                lax.ppermute(head, axis, [((i + 1) % count, i) for i in range(ends)]),
            ],
            axis=dim,
        )
    return cells


def face_flux(near_cells, far_cells, face_speed, near_wet, far_wet):
    upwind = jnp.maximum(face_speed, 0.0) * near_cells + jnp.minimum(face_speed, 0.0) * far_cells
    return near_wet * far_wet * (upwind - diffusivity * (far_cells - near_cells))


def wet_from(depth_plane, layer_stack_number):
    level_index = jnp.arange(layer_stack_number, dtype=jnp.float32)
    return (level_index[:, None, None] < depth_plane[None]).astype(jnp.float32)


def split_tracer(block_planes, layer_stack_number):
    return block_planes[: 2 * layer_stack_number].reshape(
        (2, layer_stack_number) + block_planes.shape[1:]
    )


def shards(
    thermal_deviation,
    brine_content,
    current_components,
    sea_indicator,
    flooded_layer_number,
    footprint_square_metres,
    rainfall_input,
    seam_partner_index,
):
    layer_stack_number, parallel_total_number, meridian_total_number = thermal_deviation.shape
    stacked_layer_number = (sea_indicator * flooded_layer_number).astype(jnp.float32)
    wet_area = footprint_square_metres * sea_indicator.astype(jnp.float32)
    surface = brine_content[0]
    total_area, total_fresh, salt_fresh, salt_only = lax.psum(
        (
            jnp.sum(wet_area),
            jnp.sum(wet_area * rainfall_input),
            jnp.sum(wet_area * surface * rainfall_input),
            jnp.sum(wet_area * surface),
        ),
        ("gx", "gy"),
    )
    mean_fresh = total_fresh / total_area
    balanced = rainfall_input - mean_fresh
    total_salt = salt_fresh - mean_fresh * salt_only
    virtual = -surface * balanced + total_salt / total_area
    top_row = jnp.concatenate(
        [
            thermal_deviation[:, -1, :],
            brine_content[:, -1, :],
            current_components[1][:, -1, :],
            stacked_layer_number[-1:, :],
        ],
        axis=0,
    )
    gathered = lax.all_gather(top_row, "gx", axis=1, tiled=True)
    partner_row = jnp.take(gathered, seam_partner_index, axis=1)
    partner_fields = jnp.concatenate(
        [partner_row[: 2 * layer_stack_number], partner_row[3 * layer_stack_number :]], axis=0
    )
    partner_speed = partner_row[2 * layer_stack_number : 3 * layer_stack_number]
    is_top = lax.axis_index("gy") == lax.axis_size("gy") - 1
    planes = jnp.concatenate(
        [
            thermal_deviation,
            brine_content,
            current_components[0],
            current_components[1],
            stacked_layer_number[None],
        ],
        axis=0,
    )
    zonal_padded = with_halo(planes, (("gx", 2),), 1, True)
    meridional_padded = with_halo(planes, (("gy", 1),), 1, False)
    zonal_tracer = split_tracer(zonal_padded, layer_stack_number)
    zonal_wet = wet_from(zonal_padded[4 * layer_stack_number], layer_stack_number)
    zonal_near_speed = zonal_padded[2 * layer_stack_number : 3 * layer_stack_number][..., :-1]
    halo_top = jnp.concatenate(
        [
            meridional_padded[: 2 * layer_stack_number, -1, :],
            meridional_padded[4 * layer_stack_number :, -1, :],
        ],
        axis=0,
    )
    above_fields = jnp.where(is_top, partner_fields, halo_top)
    upper_tracer_cells = jnp.concatenate(
        [
            meridional_padded[: 2 * layer_stack_number, 1:-1, :],
            above_fields[: 2 * layer_stack_number, None, :],
        ],
        axis=1,
    )
    upper_depth = jnp.concatenate(
        [
            meridional_padded[4 * layer_stack_number, 1:-1, :],
            above_fields[2 * layer_stack_number][None, :],
        ],
        axis=0,
    )
    lower_cells = meridional_padded[:, :-1, :]
    lower_tracer = split_tracer(lower_cells, layer_stack_number)
    lower_wet = wet_from(lower_cells[4 * layer_stack_number], layer_stack_number)
    upper_tracer = split_tracer(upper_tracer_cells, layer_stack_number)
    upper_wet = wet_from(upper_depth, layer_stack_number)
    north_speed = lower_cells[3 * layer_stack_number : 4 * layer_stack_number]
    carried_quantity = jnp.stack([thermal_deviation, brine_content])
    wet_cells = wet_from(stacked_layer_number, layer_stack_number)
    zonal_flux = face_flux(
        zonal_tracer[..., :-1],
        zonal_tracer[..., 1:],
        zonal_near_speed,
        zonal_wet[..., :-1],
        zonal_wet[..., 1:],
    )
    fold_speed = 0.5 * (north_speed[:, -1, :] - partner_speed)
    last_speed = jnp.where(is_top, fold_speed, north_speed[:, -1, :])
    north_speed = jnp.concatenate([north_speed[:, :-1, :], last_speed[:, None, :]], axis=1)
    meridional_flux = face_flux(lower_tracer, upper_tracer, north_speed, lower_wet, upper_wet)
    vertical = (
        wet_cells[:-1]
        * wet_cells[1:]
        * vertical_mixing
        * (carried_quantity[:, :-1] - carried_quantity[:, 1:])
    )
    zero_layer = jnp.zeros_like(vertical[:, :1])
    from_above = jnp.concatenate([zero_layer, vertical], axis=1)
    to_below = jnp.concatenate([vertical, zero_layer], axis=1)
    tendency = time_step / footprint_square_metres * (
        zonal_flux[..., :-1]
        - zonal_flux[..., 1:]
        + meridional_flux[:, :, :-1]
        - meridional_flux[:, :, 1:]
    ) + time_step * (from_above - to_below)
    updated = carried_quantity + wet_cells * tendency
    surface_next = updated[1, 0] + time_step / top_thickness * virtual * wet_cells[0]
    salinity_next = jnp.concatenate([surface_next[None], updated[1, 1:]], axis=0)
    return (updated[0], salinity_next)


def solution(mesh):
    in_specs = (
        P("groups", "gy", "gx"),
        P("groups", "gy", "gx"),
        P("groups", None, "gy", "gx"),
        P("gy", "gx"),
        P("gy", "gx"),
        P("gy", "gx"),
        P("gy", "gx"),
        P("gx"),
    )
    out_specs = (P("groups", "gy", "gx"), P("groups", "gy", "gx"))
    return jax.shard_map(shards, mesh=mesh, in_specs=in_specs, out_specs=out_specs, check_vma=False)
```

profile of v0, /device:TPU:0, one launch (start us, length us, event | category | flops | bytes accessed | tf_op | source)
XLA Modules:
  0.0 111.4 jit_solution(16813490816440808588)
XLA Ops:
  0.6 2.3 %constant_dynamic-update-slice_fusion.2 = (f32[65,64,128]{2,0,1:T(8,128)S(1)}, f32[16,64,128]{2,0,1:T(8,128)}) fusion(f32[16,64,128]{2,1,0:T(8,128)} %param.8), kind=kLoop, calls=%fused_computation.82 | loop fusion | bytes 1572864
  3.1 1.1 %constant_dynamic-update-slice_fusion.1 = (f32[65,64,128]{2,0,1:T(8,128)S(1)}, f32[16,64,128]{2,0,1:T(8,128)}) fusion(f32[65,64,128]{2,0,1:T(8,128)S(1)} %get-tuple-element.22, f32[16,64,128]{2,1,0:T(8,128)S(1)} %copy-done.2), kind=kLoop, calls=%fused_computation.81 | loop fusion | bytes 1572864
  5.0 2.9 %fusion.24 = (f32[65,64,1]{2,0,1:T(8,128)}, f32[65,64,1]{2,0,1:T(8,128)}) fusion(f32[65,64,128]{2,0,1:T(8,128)S(1)} %dynamic-update-slice.4), kind=kLoop, calls=%fused_computation.87 | loop fusion | bytes 66560 | tf_op jit(solution)/shard_map/slice | solution.py:17
  7.9 3.1 %copy.160 = f32[65,64,1]{0,1,2:T(8,128)} copy(f32[65,64,1]{2,0,1:T(8,128)} %get-tuple-element.14) | data formatting | bytes 33280 | tf_op jit(solution)/shard_map/slice | solution.py:17
  11.0 3.1 %collective-permute-start = (f32[65,64,1]{0,1,2:T(8,128)}, f32[65,64,1]{0,1,2:T(8,128)}, u32[]{:S(2)}, u32[]{:S(2)}) collective-permute-start(f32[65,64,1]{0,1,2:T(8,128)} %copy.160), channel_id=1, source_target_pairs={{0,4},{4,8},{8,12},{12,0},{1,5},{5,9},{9,13},{13,1},{2,6},{6,10},{... | collective-permute-start | bytes 49928 | tf_op jit(solution)/shard_map/ppermute | solution.py:20
  14.0 3.1 %copy.161 = f32[65,64,1]{0,1,2:T(8,128)} copy(f32[65,64,1]{2,0,1:T(8,128)} %get-tuple-element.15) | data formatting | bytes 33280 | tf_op jit(solution)/shard_map/slice | solution.py:16
  17.1 2.1 %collective-permute-start.1 = (f32[65,64,1]{0,1,2:T(8,128)}, f32[65,64,1]{0,1,2:T(8,128)}, u32[]{:S(2)}, u32[]{:S(2)}) collective-permute-start(f32[65,64,1]{0,1,2:T(8,128)} %copy.161), channel_id=1, source_target_pairs={{4,0},{8,4},{12,8},{0,12},{5,1},{9,5},{13,9},{1,13},{6,2},{10,6},{... | collective-permute-start | bytes 49928 | tf_op jit(solution)/shard_map/ppermute | solution.py:22
  19.8 1.3 %collective-permute-start.2 = (f32[65,1,128]{2,0,1:T(8,128)}, f32[65,1,128]{2,0,1:T(8,128)}, u32[]{:S(2)}, u32[]{:S(2)}) collective-permute-start(f32[65,1,128]{2,0,1:T(8,128)} %get-tuple-element.17), channel_id=1, source_target_pairs={{1,0},{2,1},{3,2},{5,4},{6,5},{7,6},{9,8},{10,9},{11,10},{13,12},{... | collective-permute-start | bytes 99848 | tf_op jit(solution)/shard_map/ppermute | solution.py:22
  21.1 3.6 %collective-permute-start.3 = (f32[65,1,128]{2,0,1:T(8,128)}, f32[65,1,128]{2,0,1:T(8,128)}, u32[]{:S(2)}, u32[]{:S(2)}) collective-permute-start(f32[65,1,128]{2,0,1:T(8,128)} %get-tuple-element.16), channel_id=1, source_target_pairs={{0,1},{1,2},{2,3},{4,5},{5,6},{6,7},{8,9},{9,10},{10,11},{12,13},{... | collective-permute-start | bytes 99848 | tf_op jit(solution)/shard_map/ppermute | solution.py:20
  24.7 1.3 %copy.203 = f32[1,16,64,128]{3,1,2,0:T(8,128)S(1)} copy(f32[1,16,64,128]{3,2,1,0:T(8,128)} %copy-done.5) | data formatting | bytes 1048576
  27.3 1.1 pad_maximum_fusion.6
  30.6 13.3 %all_gather.3 = f32[49,512]{1,0:T(8,128)S(1)} all-gather(f32[49,128]{1,0:T(8,128)S(1)} %pad_maximum_fusion.11), channel_id=1, replica_groups=mesh['groups'=2,'gx'=4,'gy'=4] {'gx'}, dimensions={1}, use_global_device_ids=true | all-gather | bytes 125440 | tf_op jit(solution)/shard_map/all_gather | solution.py:81
  45.4 1.6 %gather_fusion = f32[128,49]{1,0:T(8,128)S(1)} fusion(f32[49,512]{0,1:T(8,128)} %copy.172, s32[1024]{0:T(1024)S(1)} %pad_clamp_fusion), kind=kCustom, calls=%fused_computation | custom fusion | bytes 50688 | tf_op jit(solution)/shard_map/jit(_take)/gather | solution.py:82
  47.7 2.0 %fusion.12 = f32[15,64,128]{2,1,0:T(8,128)} fusion(f32[16,64,128]{2,1,0:T(8,128)} %fusion.11), kind=kLoop, calls=%fused_computation.45 | loop fusion | flops 245760 | bytes 1474560 | tf_op jit(solution)/shard_map/mul | solution.py:145
  50.6 1.4 %select_bitcast_fusion = f32[49,128]{1,0:T(8,128)} fusion(f32[128,49]{0,1:T(8,128)} %copy.173, pred[128]{0:T(512)(128)(4,1)} %compare_and_fusion), kind=kLoop, calls=%fused_computation.68 | loop fusion | flops 6272 | bytes 50304 | tf_op jit(solution)/shard_map/jit(_take)/select_n | solution.py:82
  52.6 2.1 %fusion.7 = f32[2,15,64,128]{3,2,1,0:T(8,128)} fusion(f32[1,16,64,128]{3,2,1,0:T(8,128)S(1)} %bitcast.78, f32[1,16,64,128]{3,2,1,0:T(8,128)S(1)} %bitcast.76, f32[15,64,128]{2,1,0:T(8,128)} %fusion.12), kind=kLoop, calls=%fused_computation.26 | loop fusion | flops 983040 | bytes 2523136 | tf_op jit(solution)/shard_map/mul | solution.py:145
  55.4 30.3 %all-reduce.2 = (f32[]{:T(128)}, f32[]{:T(128)}, f32[]{:T(128)}, f32[]{:T(128)}) all-reduce(f32[]{:T(128)} %get-tuple-element.3, f32[]{:T(128)} %get-tuple-element.4, f32[]{:T(128)} %get-tuple-element.5, f32[]{:T(128)} %get-tuple-element.2), channel_id=1, replica_groups=mesh['groups'=2,'gx'=4,'gy'=4] {'gx','gy'}, use_global_device_ids=true, to_apply=%region_5.0 | all-reduce | flops 4 | bytes 32 | tf_op jit(solution)/shard_map/psum | solution.py:59
  88.9 3.0 %copy.162 = f32[65,64,1]{2,0,1:T(8,128)} copy(f32[65,64,1]{0,1,2:T(8,128)} %collective-permute-done) | data formatting | bytes 33280 | tf_op jit(solution)/shard_map/ppermute | solution.py:20
  91.9 3.0 %copy.163 = f32[65,64,1]{2,0,1:T(8,128)} copy(f32[65,64,1]{0,1,2:T(8,128)} %collective-permute-done.1) | data formatting | bytes 33280 | tf_op jit(solution)/shard_map/ppermute | solution.py:22
  94.9 1.5 %pad_maximum_fusion.8 = f32[1,64,130]{2,0,1:T(1,128)S(1)} fusion(f32[65,64,1]{2,0,1:T(8,128)} %copy.163, f32[65,64,128]{2,0,1:T(8,128)S(1)} %dynamic-update-slice.4, f32[65,64,1]{2,0,1:T(8,128)} %copy.162), kind=kLoop, calls=%fused_computation.48 | loop fusion | flops 16640 | bytes 2196480 | tf_op jit(solution)/shard_map/slice | solution.py:101
  97.5 0.9 pad_maximum_fusion
  99.2 1.2 %copy.167 = f32[32,64,130]{2,1,0:T(8,128)S(1)} copy(f32[32,64,130]{2,0,1:T(8,128)S(1)} %pad_maximum_fusion) | data formatting | bytes 2129920 | tf_op jit(solution)/shard_map/slice | solution.py:40
  101.8 1.1 subtract_multiply_fusion
  106.6 0.9 pad_maximum_fusion.4
  (85 shorter events, 20.0 us)
Async XLA Ops:
  0.6 2.3 %copy-start.8 = (f32[2,16,64,128]{3,2,1,0:T(8,128)S(1)}, f32[2,16,64,128]{3,2,1,0:T(8,128)}, u32[]{:S(2)}) copy-start(f32[2,16,64,128]{3,2,1,0:T(8,128)} %param.10) | copy-start | bytes 3145732
  0.6 2.4 %copy-start.2 = (f32[16,64,128]{2,1,0:T(8,128)S(1)}, f32[16,64,128]{2,1,0:T(8,128)}, u32[]{:S(2)}) copy-start(f32[16,64,128]{2,1,0:T(8,128)} %param.9) | copy-start | bytes 1572868
  3.0 1.8 %copy-start.5 = (f32[1,16,64,128]{3,2,1,0:T(8,128)}, f32[1,16,64,128]{3,2,1,0:T(8,128)S(1)}, u32[]{:S(2)}) copy-start(f32[1,16,64,128]{3,2,1,0:T(8,128)S(1)} %get-tuple-element.19) | copy-start | bytes 1572868
  3.0 1.8 %copy-start.11 = (s32[64,128]{1,0:T(8,128)S(1)}, s32[64,128]{1,0:T(8,128)}, u32[]{:S(2)}) copy-start(s32[64,128]{1,0:T(8,128)} %param.11) | copy-start | bytes 98308
  3.0 1.8 %copy-start.13 = (s32[64,128]{1,0:T(8,128)S(1)}, s32[64,128]{1,0:T(8,128)}, u32[]{:S(2)}) copy-start(s32[64,128]{1,0:T(8,128)} %param.12) | copy-start | bytes 98308
  11.0 15.1 %copy-start.14 = (s32[128]{0:T(128)S(1)}, s32[128]{0:T(128)}, u32[]{:S(2)}) copy-start(s32[128]{0:T(128)} %param.15) | copy-start | bytes 1540
  11.0 16.3 %copy-start.3 = (f32[16,64,128]{2,1,0:T(8,128)S(1)}, f32[16,64,128]{2,1,0:T(8,128)}, u32[]{:S(2)}) copy-start(f32[16,64,128]{2,1,0:T(8,128)} %param.8) | copy-start | bytes 1572868
  11.0 77.9 %collective-permute-start = (f32[65,64,1]{0,1,2:T(8,128)}, f32[65,64,1]{0,1,2:T(8,128)}, u32[]{:S(2)}, u32[]{:S(2)}) collective-permute-start(f32[65,64,1]{0,1,2:T(8,128)} %copy.160), channel_id=1, source_target_pairs={{0,4},{4,8},{8,12},{12,0},{1,5},{5,9},{9,13},{13,1},{2,6},{6,10},{... | collective-permute-start | bytes 49928 | tf_op jit(solution)/shard_map/ppermute | solution.py:20
  17.1 74.8 %collective-permute-start.1 = (f32[65,64,1]{0,1,2:T(8,128)}, f32[65,64,1]{0,1,2:T(8,128)}, u32[]{:S(2)}, u32[]{:S(2)}) collective-permute-start(f32[65,64,1]{0,1,2:T(8,128)} %copy.161), channel_id=1, source_target_pairs={{4,0},{8,4},{12,8},{0,12},{5,1},{9,5},{13,9},{1,13},{6,2},{10,6},{... | collective-permute-start | bytes 49928 | tf_op jit(solution)/shard_map/ppermute | solution.py:22
  19.8 83.1 %collective-permute-start.2 = (f32[65,1,128]{2,0,1:T(8,128)}, f32[65,1,128]{2,0,1:T(8,128)}, u32[]{:S(2)}, u32[]{:S(2)}) collective-permute-start(f32[65,1,128]{2,0,1:T(8,128)} %get-tuple-element.17), channel_id=1, source_target_pairs={{1,0},{2,1},{3,2},{5,4},{6,5},{7,6},{9,8},{10,9},{11,10},{13,12},{... | collective-permute-start | bytes 99848 | tf_op jit(solution)/shard_map/ppermute | solution.py:22
  21.1 83.2 %collective-permute-start.3 = (f32[65,1,128]{2,0,1:T(8,128)}, f32[65,1,128]{2,0,1:T(8,128)}, u32[]{:S(2)}, u32[]{:S(2)}) collective-permute-start(f32[65,1,128]{2,0,1:T(8,128)} %get-tuple-element.16), channel_id=1, source_target_pairs={{0,1},{1,2},{2,3},{4,5},{5,6},{6,7},{8,9},{9,10},{10,11},{12,13},{... | collective-permute-start | bytes 99848 | tf_op jit(solution)/shard_map/ppermute | solution.py:20
  26.1 3.8 %copy-start.9 = (f32[1,16,64,128]{3,1,2,0:T(8,128)}, f32[1,16,64,128]{3,1,2,0:T(8,128)S(1)}, u32[]{:S(2)}) copy-start(f32[1,16,64,128]{3,1,2,0:T(8,128)S(1)} %copy.203) | copy-start | bytes 1572868
  47.7 7.0 %copy-start.10 = (f32[64,128]{1,0:T(8,128)S(1)}, f32[64,128]{1,0:T(8,128)}, u32[]{:S(2)}) copy-start(f32[64,128]{1,0:T(8,128)} %param.14) | copy-start | bytes 98308
  94.9 1.8 %copy-start = (f32[65,64,1]{2,0,1:T(8,128)S(1)}, f32[65,64,1]{2,0,1:T(8,128)}, u32[]{:S(2)}) copy-start(f32[65,64,1]{2,0,1:T(8,128)} %copy.162) | copy-start | bytes 49924
  94.9 2.5 %copy-start.1 = (f32[65,64,1]{2,0,1:T(8,128)S(1)}, f32[65,64,1]{2,0,1:T(8,128)}, u32[]{:S(2)}) copy-start(f32[65,64,1]{2,0,1:T(8,128)} %copy.163) | copy-start | bytes 49924
  101.8 2.5 %slice-start = ((f32[49,128]{1,0:T(8,128)}), f32[32,128]{1,0:T(8,128)S(1)}, s32[]{:S(2)}) async-start(f32[49,128]{1,0:T(8,128)} %select_bitcast_fusion), calls=%async_computation | async-start | bytes 32768 | tf_op jit(solution)/shard_map/slice | solution.py:84
  101.8 2.5 %slice-start.1 = ((f32[49,128]{1,0:T(8,128)}), f32[1,128]{1,0:T(1,128)S(1)}, s32[]{:S(2)}) async-start(f32[49,128]{1,0:T(8,128)} %select_bitcast_fusion), calls=%async_computation.1 | async-start | bytes 1024 | tf_op jit(solution)/shard_map/slice | solution.py:84
  104.3 1.1 copy-start.12
  106.4 1.2 %copy-start.6 = (f32[32,64,128]{2,1,0:T(8,128)S(1)}, f32[32,64,128]{2,1,0:T(8,128)}, u32[]{:S(2)}) copy-start(f32[32,64,128]{2,1,0:T(8,128)} %pad_maximum_fusion.6) | copy-start | bytes 3145732
  106.4 1.2 %slice-start.2 = ((f32[33,128]{1,0:T(8,128)}), f32[32,128]{1,0:T(8,128)S(1)}, s32[]{:S(2)}) async-start(f32[33,128]{1,0:T(8,128)} %copy-done.12), calls=%async_computation.2 | async-start | bytes 32768 | tf_op jit(solution)/shard_map/slice | solution.py:114
  107.6 1.0 copy-start.4
  107.6 1.4 %copy-start.7 = (f32[2,15,64,128]{3,2,1,0:T(8,128)S(1)}, f32[2,15,64,128]{3,2,1,0:T(8,128)}, u32[]{:S(2)}) copy-start(f32[2,15,64,128]{3,2,1,0:T(8,128)} %fusion.7) | copy-start | bytes 2949124
where the time goes:
time: 112 us; the launch traced here: 111 us
  blocking collectives  43.6 us (39%)
  local copies, waits for them, and re-layouts  32.9 us (29%)
  other arithmetic  20.6 us (18%)
  starting transfers between devices  10.1 us (9%)
  between operations  4.18 us (4%)
    psum x1, blocking collectives, shards(): lax.psum((jnp.sum(wet_area), jnp.sum(wet_area * rainfall_input), jnp.sum(...  30.3 us
    all_gather x1, blocking collectives, shards(): gathered = lax.all_gather(top_row, 'gx', axis=1, tiled=True)  13.3 us
    unnamed x37, local copies, waits for them, and re-layouts  7.21 us
    ppermute x2, starting transfers between devices, with_halo(): lax.ppermute(tail, axis, [(i, (i + 1) % count) for i in range(ends)])  6.7 us
    slice x3, local copies, waits for them, and re-layouts, with_halo(): lax.slice_in_dim(cells, cells.shape[dim] - width, cells.shape[dim], axis=...  6.57 us
    mul x2, other arithmetic, shards(): wet_cells[:-1] * wet_cells[1:] * vertical_mixing  4.14 us
    ppermute x2, starting transfers between devices, with_halo(): lax.ppermute(head, axis, [((i + 1) % count, i) for i in range(ends)])  3.37 us
    slice x1, local copies, waits for them, and re-layouts, with_halo(): head = lax.slice_in_dim(cells, 0, width, axis=dim)  3.07 us
  transfers between devices with their start and end apart: 4, of which 0 were waited for; matrix products, arithmetic and copies ran while one was open for 32% of the time, Pallas kernels for 0%

commit v1 on v0

--- a/solution.py
+++ b/solution.py
@@ -78,7 +78,14 @@
         ],
         axis=0,
     )
-    gathered = lax.all_gather(top_row, "gx", axis=1, tiled=True)
+    ways = lax.axis_size("gx")
+    pieces = [top_row]
+    for far in range(1, ways):
+        pieces.append(
+            lax.ppermute(pieces[far - 1], "gx", [(d, (d - 1) % ways) for d in range(ways)])
+        )
+    line = jnp.concatenate(pieces, axis=1)
+    gathered = jnp.roll(line, lax.axis_index("gx") * top_row.shape[1], axis=1)
     partner_row = jnp.take(gathered, seam_partner_index, axis=1)
     partner_fields = jnp.concatenate(
         [partner_row[: 2 * layer_stack_number], partner_row[3 * layer_stack_number :]], axis=0

time: 112 us -> 93.3 us (0.83)
  blocking collectives: 43.6 us -> 34.3 us
  other arithmetic: 20.6 us -> 12.4 us
  local copies, waits for them, and re-layouts: 32.9 us -> 26.6 us
  waiting for transfers between devices: 0.01 us -> 3.08 us
  starting transfers between devices: 10.1 us -> 11.9 us
    all_gather x1 -> x0, blocking collectives: 13.3 us -> none  [shards(): gathered = lax.all_gather(top_row, 'gx', axis=1, tiled=True)]
    ppermute x0 -> x3, starting transfers between devices: none -> 6.22 us  [shards(): lax.ppermute(pieces[far - 1], 'gx', [(d, (d - 1) % ways) for d in range(w...]
    psum x1, blocking collectives: 30.3 us -> 34.3 us  [shards(): lax.psum((jnp.sum(wet_area), jnp.sum(wet_area * rainfall_input), jnp.sum(...]
    ppermute x0 -> x3, waiting for transfers between devices: none -> 3.07 us  [shards(): lax.ppermute(pieces[far - 1], 'gx', [(d, (d - 1) % ways) for d in range(w...]
    mul x2, other arithmetic: 4.14 us -> 1.15 us  [shards(): wet_cells[:-1] * wet_cells[1:] * vertical_mixing]
    ppermute x2, starting transfers between devices: 6.7 us -> 3.98 us  [with_halo(): lax.ppermute(tail, axis, [(i, (i + 1) % count) for i in range(ends)])]
    slice x2 -> x1, other arithmetic: 2.16 us -> 0.05 us  [shards(): north_speed[:, :-1, :]]
    squeeze x3 -> x1, local copies, waits for them, and re-layouts: 2.12 us -> 0.04 us  [shards(): current_components[1]]
  transfers between devices with their start and end apart: 4 -> 7, of which waited for: 0 -> 2; matrix products, arithmetic and copies ran while one was open for 32% -> 31% of each run, Pallas kernels for 0% -> 0%
where the time goes in v1:
time: 93.3 us; the launch traced here: 92.8 us
  blocking collectives  34.3 us (37%)
  local copies, waits for them, and re-layouts  26.6 us (29%)
  other arithmetic  12.4 us (13%)
  starting transfers between devices  11.9 us (13%)
  between operations  4.38 us (5%)
  waiting for transfers between devices  3.08 us (3%)
    psum x1, blocking collectives, shards(): lax.psum((jnp.sum(wet_area), jnp.sum(wet_area * rainfall_input), jnp.sum(...  34.3 us
    unnamed x44, local copies, waits for them, and re-layouts  6.3 us
    ppermute x3, starting transfers between devices, shards(): lax.ppermute(pieces[far - 1], 'gx', [(d, (d - 1) % ways) for d in range(w...  6.22 us
    slice x2, local copies, waits for them, and re-layouts, with_halo(): lax.slice_in_dim(cells, cells.shape[dim] - width, cells.shape[dim], axis=...  6.16 us
    ppermute x2, starting transfers between devices, with_halo(): lax.ppermute(tail, axis, [(i, (i + 1) % count) for i in range(ends)])  3.98 us
    ppermute x1, local copies, waits for them, and re-layouts, with_halo(): lax.ppermute(head, axis, [((i + 1) % count, i) for i in range(ends)])  3.78 us
    ppermute x1, local copies, waits for them, and re-layouts, with_halo(): lax.ppermute(tail, axis, [(i, (i + 1) % count) for i in range(ends)])  3.74 us
    concatenate x2, other arithmetic, with_halo(): jnp.concatenate([lax.ppermute(tail, axis, [(i, (i + 1) % count) for i in...  3.71 us
  transfers between devices with their start and end apart: 7, of which 2 were waited for; matrix products, arithmetic and copies ran while one was open for 31% of the time, Pallas kernels for 0%

profile of v1, /device:TPU:0, one launch (start us, length us, event | category | flops | bytes accessed | tf_op | source)
XLA Modules:
  0.0 92.8 jit_solution(832288617540467360)
XLA Ops:
  0.7 1.2 %constant_dynamic-update-slice_fusion.2 = f32[65,64,128]{2,1,0:T(8,128)S(1)} fusion(f32[16,64,128]{2,1,0:T(8,128)} %param.8), kind=kLoop, calls=%fused_computation.68 | loop fusion | bytes 1048576
  1.9 1.2 %constant_dynamic-update-slice_fusion.1 = f32[65,64,128]{2,1,0:T(8,128)S(1)} fusion(f32[65,64,128]{2,1,0:T(8,128)S(1)} %constant_dynamic-update-slice_fusion.2, f32[16,64,128]{2,1,0:T(8,128)} %param.9), kind=kLoop, calls=%fused_computation.67 | loop fusion | bytes 1048576
  3.2 2.4 %collective-permute-start.6 = (f32[65,1,128]{2,1,0:T(1,128)S(1)}, f32[65,1,128]{2,1,0:T(1,128)S(1)}, u32[]{:S(2)}, u32[]{:S(2)}) collective-permute-start(f32[65,1,128]{2,1,0:T(1,128)S(1)} %get-tuple-element.17), channel_id=1, source_target_pairs={{0,1},{1,2},{2,3},{4,5},{5,6},{6,7},{8,9},{9,10},{10,11},{12,13},{... | collective-permute-start | bytes 99848 | tf_op jit(solution)/shard_map/ppermute | solution.py:20
  6.4 4.4 %collective-permute-start.2 = (f32[49,128]{1,0:T(8,128)}, f32[49,128]{1,0:T(8,128)S(1)}, u32[]{:S(2)}, u32[]{:S(2)}) collective-permute-start(f32[49,128]{1,0:T(8,128)} %get-tuple-element.22), channel_id=1, source_target_pairs={{0,12},{4,0},{8,4},{12,8},{1,13},{5,1},{9,5},{13,9},{2,14},{6,2},{... | collective-permute-start | bytes 75272 | tf_op jit(solution)/shard_map/ppermute | solution.py:85
  10.8 1.3 %collective-permute-start.5 = (f32[65,1,128]{2,1,0:T(1,128)S(1)}, f32[65,1,128]{2,1,0:T(1,128)}, u32[]{:S(2)}, u32[]{:S(2)}) collective-permute-start(f32[65,1,128]{2,1,0:T(1,128)S(1)} %get-tuple-element.16), channel_id=1, source_target_pairs={{1,0},{2,1},{3,2},{5,4},{6,5},{7,6},{9,8},{10,9},{11,10},{13,12},{... | collective-permute-start | bytes 99848 | tf_op jit(solution)/shard_map/ppermute | solution.py:22
  12.1 2.8 %fusion.23 = (f32[65,64,1]{2,1,0:T(8,128)}, f32[65,64,1]{2,1,0:T(8,128)}) fusion(f32[65,64,128]{2,1,0:T(8,128)S(1)} %get-tuple-element.12), kind=kLoop, calls=%fused_computation.89 | loop fusion | bytes 66560 | tf_op jit(solution)/shard_map/slice | solution.py:17
  14.9 2.8 %copy.92 = f32[65,64,1]{0,1,2:T(8,128)S(1)} copy(f32[65,64,1]{2,1,0:T(8,128)} %get-tuple-element.15) | data formatting | bytes 33280 | tf_op jit(solution)/shard_map/slice | solution.py:16
  18.2 3.3 %copy.91 = f32[65,64,1]{0,1,2:T(8,128)} copy(f32[65,64,1]{2,1,0:T(8,128)} %get-tuple-element.14) | data formatting | bytes 33280 | tf_op jit(solution)/shard_map/slice | solution.py:17
  21.5 1.6 %collective-permute-start = (f32[65,64,1]{0,1,2:T(8,128)}, f32[65,64,1]{0,1,2:T(8,128)}, u32[]{:S(2)}, u32[]{:S(2)}) collective-permute-start(f32[65,64,1]{0,1,2:T(8,128)} %copy.91), channel_id=1, source_target_pairs={{0,4},{4,8},{8,12},{12,0},{1,5},{5,9},{9,13},{13,1},{2,6},{6,10},{... | collective-permute-start | bytes 49928 | tf_op jit(solution)/shard_map/ppermute | solution.py:20
  23.1 1.1 %pad_maximum_fusion.6 = f32[32,64,128]{2,1,0:T(8,128)} fusion(f32[16,64,128]{2,1,0:T(8,128)S(1)} %copy-done.2, f32[16,64,128]{2,1,0:T(8,128)S(1)} %copy-done.3), kind=kLoop, calls=%fused_computation.21 | loop fusion | flops 262144 | bytes 2097152 | tf_op jit(solution)/shard_map/concatenate | solution.py:95
  24.3 0.8 copy-done.5
  25.8 1.1 %fusion.7 = f32[2,15,64,128]{3,2,1,0:T(8,128)} fusion(f32[1,16,64,128]{3,2,1,0:T(8,128)S(1)} %bitcast.70, f32[1,16,64,128]{3,2,1,0:T(8,128)S(1)} %bitcast.68, f32[15,64,128]{2,1,0:T(8,128)S(1)} %fusion.10), kind=kLoop, calls=%fused_computation.26 | loop fusion | flops 983040 | bytes 2523136 | tf_op jit(solution)/shard_map/mul | solution.py:152
  26.9 34.3 %all-reduce.2 = (f32[]{:T(128)}, f32[]{:T(128)}, f32[]{:T(128)}, f32[]{:T(128)}) all-reduce(f32[]{:T(128)} %get-tuple-element.3, f32[]{:T(128)} %get-tuple-element.4, f32[]{:T(128)} %get-tuple-element.5, f32[]{:T(128)} %get-tuple-element.2), channel_id=1, replica_groups=mesh['groups'=2,'gx'=4,'gy'=4] {'gx','gy'}, use_global_device_ids=true, to_apply=%region_5.0 | all-reduce | flops 4 | bytes 32 | tf_op jit(solution)/shard_map/psum | solution.py:59
  64.4 3.8 %copy.94 = f32[65,64,1]{2,1,0:T(8,128)} copy(f32[65,64,1]{0,1,2:T(8,128)} %collective-permute-done.1) | data formatting | bytes 33280 | tf_op jit(solution)/shard_map/ppermute | solution.py:22
  68.2 3.7 %copy.93 = f32[65,64,1]{2,1,0:T(8,128)} copy(f32[65,64,1]{0,1,2:T(8,128)} %collective-permute-done) | data formatting | bytes 33280 | tf_op jit(solution)/shard_map/ppermute | solution.py:20
  71.9 2.6 %pad_maximum_fusion = f32[32,64,130]{2,1,0:T(8,128)S(1)} fusion(f32[65,64,1]{2,1,0:T(8,128)} %copy.94, f32[65,64,128]{2,1,0:T(8,128)S(1)} %get-tuple-element.12, f32[65,64,1]{2,1,0:T(8,128)} %copy.93), kind=kLoop, calls=%fused_computation.1 | loop fusion | flops 532480 | bytes 3228160 | tf_op jit(solution)/shard_map/concatenate | solution.py:18
  75.8 2.1 %subtract_multiply_fusion = f32[2,16,64,129]{3,2,1,0:T(8,128)} fusion(f32[2,16,64,130]{3,2,1,0:T(8,128)S(1)} %bitcast.67, f32[16,64,129]{2,1,0:T(8,128)S(1)} %get-tuple-element.25, f32[16,64,129]{2,1,0:T(8,128)S(1)} %get-tuple-element.10, f32[16,64,129]{2,1,0:T(8,128)S(1)} %get-tuple-element.24), kind=kLoop, calls=%fused_computation.3 | loop fusion | flops 1849344 | bytes 4755456 | tf_op jit(solution)/shard_map/mul | solution.py:31
  78.0 1.1 %pad_maximum_fusion.3 = f32[32,65,128]{2,1,0:T(8,128)} fusion(f32[65,64,128]{2,1,0:T(8,128)S(1)} %get-tuple-element.12, f32[65,1,128]{2,1,0:T(1,128)S(1)} %collective-permute-done.6), kind=kLoop, calls=%fused_computation.9 | loop fusion | flops 266240 | bytes 3228160 | tf_op jit(solution)/shard_map/concatenate | solution.py:18
  80.8 1.0 %collective-permute-done.3 = f32[49,128]{1,0:T(8,128)S(1)} collective-permute-done((f32[49,128]{1,0:T(8,128)S(1)}, f32[49,128]{1,0:T(8,128)S(1)}, u32[]{:S(2)}, u32[]{:S(2)}) %collective-permute-start.3) | collective-permute-done | bytes 25120 | tf_op jit(solution)/shard_map/ppermute | solution.py:85
  81.8 1.8 %collective-permute-start.4 = (f32[49,128]{1,0:T(8,128)S(1)}, f32[49,128]{1,0:T(8,128)S(1)}, u32[]{:S(2)}, u32[]{:S(2)}) collective-permute-start(f32[49,128]{1,0:T(8,128)S(1)} %collective-permute-done.3), channel_id=1, source_target_pairs={{0,12},{4,0},{8,4},{12,8},{1,13},{5,1},{9,5},{13,9},{2,14},{6,2},{... | collective-permute-start | bytes 75272 | tf_op jit(solution)/shard_map/ppermute | solution.py:85
  83.6 2.1 %collective-permute-done.4 = f32[49,128]{1,0:T(8,128)S(1)} collective-permute-done((f32[49,128]{1,0:T(8,128)S(1)}, f32[49,128]{1,0:T(8,128)S(1)}, u32[]{:S(2)}, u32[]{:S(2)}) %collective-permute-start.4) | collective-permute-done | bytes 25120 | tf_op jit(solution)/shard_map/ppermute | solution.py:85
  88.7 1.3 %copy-done.4 = f32[2,16,64,129]{3,2,1,0:T(8,128)S(1)} copy-done((f32[2,16,64,129]{3,2,1,0:T(8,128)S(1)}, f32[2,16,64,129]{3,2,1,0:T(8,128)}, u32[]{:S(2)}) %copy-start.4) | copy-done | bytes 1056792
  91.0 0.8 slice_bitcast_fusion
  91.9 0.8 pad_maximum_fusion.9
  (93 shorter events, 9.0 us)
Async XLA Ops:
  0.6 2.4 %copy-start.10 = (f32[2,16,64,128]{3,2,1,0:T(8,128)S(1)}, f32[2,16,64,128]{3,2,1,0:T(8,128)}, u32[]{:S(2)}) copy-start(f32[2,16,64,128]{3,2,1,0:T(8,128)} %param.10) | copy-start | bytes 3145732
  0.6 2.5 %copy-start.12 = (s32[64,128]{1,0:T(8,128)S(1)}, s32[64,128]{1,0:T(8,128)}, u32[]{:S(2)}) copy-start(s32[64,128]{1,0:T(8,128)} %param.11) | copy-start | bytes 98308
  0.7 2.5 %copy-start.14 = (s32[64,128]{1,0:T(8,128)S(1)}, s32[64,128]{1,0:T(8,128)}, u32[]{:S(2)}) copy-start(s32[64,128]{1,0:T(8,128)} %param.12) | copy-start | bytes 98308
  1.8 3.9 %copy-start.2 = (f32[16,64,128]{2,1,0:T(8,128)S(1)}, f32[16,64,128]{2,1,0:T(8,128)}, u32[]{:S(2)}) copy-start(f32[16,64,128]{2,1,0:T(8,128)} %param.9) | copy-start | bytes 1572868
  1.8 3.9 %copy-start.3 = (f32[16,64,128]{2,1,0:T(8,128)S(1)}, f32[16,64,128]{2,1,0:T(8,128)}, u32[]{:S(2)}) copy-start(f32[16,64,128]{2,1,0:T(8,128)} %param.8) | copy-start | bytes 1572868
  3.2 74.7 %collective-permute-start.6 = (f32[65,1,128]{2,1,0:T(1,128)S(1)}, f32[65,1,128]{2,1,0:T(1,128)S(1)}, u32[]{:S(2)}, u32[]{:S(2)}) collective-permute-start(f32[65,1,128]{2,1,0:T(1,128)S(1)} %get-tuple-element.17), channel_id=1, source_target_pairs={{0,1},{1,2},{2,3},{4,5},{5,6},{6,7},{8,9},{9,10},{10,11},{12,13},{... | collective-permute-start | bytes 99848 | tf_op jit(solution)/shard_map/ppermute | solution.py:20
  6.4 71.5 %collective-permute-start.2 = (f32[49,128]{1,0:T(8,128)}, f32[49,128]{1,0:T(8,128)S(1)}, u32[]{:S(2)}, u32[]{:S(2)}) collective-permute-start(f32[49,128]{1,0:T(8,128)} %get-tuple-element.22), channel_id=1, source_target_pairs={{0,12},{4,0},{8,4},{12,8},{1,13},{5,1},{9,5},{13,9},{2,14},{6,2},{... | collective-permute-start | bytes 75272 | tf_op jit(solution)/shard_map/ppermute | solution.py:85
  10.8 68.3 %collective-permute-start.5 = (f32[65,1,128]{2,1,0:T(1,128)S(1)}, f32[65,1,128]{2,1,0:T(1,128)}, u32[]{:S(2)}, u32[]{:S(2)}) collective-permute-start(f32[65,1,128]{2,1,0:T(1,128)S(1)} %get-tuple-element.16), channel_id=1, source_target_pairs={{1,0},{2,1},{3,2},{5,4},{6,5},{7,6},{9,8},{10,9},{11,10},{13,12},{... | collective-permute-start | bytes 99848 | tf_op jit(solution)/shard_map/ppermute | solution.py:22
  14.9 8.2 %copy-start.16 = (s32[128]{0:T(128)S(1)}, s32[128]{0:T(128)}, u32[]{:S(2)}) copy-start(s32[128]{0:T(128)} %param.15) | copy-start | bytes 1540
  17.7 46.7 %collective-permute-start.1 = (f32[65,64,1]{0,1,2:T(8,128)S(1)}, f32[65,64,1]{0,1,2:T(8,128)}, u32[]{:S(2)}, u32[]{:S(2)}) collective-permute-start(f32[65,64,1]{0,1,2:T(8,128)S(1)} %copy.92), channel_id=1, source_target_pairs={{4,0},{8,4},{12,8},{0,12},{5,1},{9,5},{13,9},{1,13},{6,2},{10,6},{... | collective-permute-start | bytes 49928 | tf_op jit(solution)/shard_map/ppermute | solution.py:22
  21.5 3.6 %copy-start.15 = (f32[64,128]{1,0:T(8,128)S(1)}, f32[64,128]{1,0:T(8,128)}, u32[]{:S(2)}) copy-start(f32[64,128]{1,0:T(8,128)} %param.13) | copy-start | bytes 98308
  21.5 46.7 %collective-permute-start = (f32[65,64,1]{0,1,2:T(8,128)}, f32[65,64,1]{0,1,2:T(8,128)}, u32[]{:S(2)}, u32[]{:S(2)}) collective-permute-start(f32[65,64,1]{0,1,2:T(8,128)} %copy.91), channel_id=1, source_target_pairs={{0,4},{4,8},{8,12},{12,0},{1,5},{5,9},{9,13},{13,1},{2,6},{6,10},{... | collective-permute-start | bytes 49928 | tf_op jit(solution)/shard_map/ppermute | solution.py:20
  23.1 2.0 %copy-start.11 = (f32[64,128]{1,0:T(8,128)S(1)}, f32[64,128]{1,0:T(8,128)}, u32[]{:S(2)}) copy-start(f32[64,128]{1,0:T(8,128)} %param.14) | copy-start | bytes 98308
  24.2 0.8 copy-start.5
  71.9 2.6 %copy-start = (f32[65,64,1]{2,1,0:T(8,128)S(1)}, f32[65,64,1]{2,1,0:T(8,128)}, u32[]{:S(2)}) copy-start(f32[65,64,1]{2,1,0:T(8,128)} %copy.93) | copy-start | bytes 49924
  71.9 2.9 %copy-start.1 = (f32[65,64,1]{2,1,0:T(8,128)S(1)}, f32[65,64,1]{2,1,0:T(8,128)}, u32[]{:S(2)}) copy-start(f32[65,64,1]{2,1,0:T(8,128)} %copy.94) | copy-start | bytes 49924
  75.8 2.2 %copy-start.13 = (f32[49,1024]{1,0:T(8,128)S(1)}, f32[49,1024]{1,0:T(8,128)}, u32[]{:S(2)}) copy-start(f32[49,1024]{1,0:T(8,128)} %get-tuple-element.23) | copy-start | bytes 602116
  77.9 3.9 %collective-permute-start.3 = (f32[49,128]{1,0:T(8,128)S(1)}, f32[49,128]{1,0:T(8,128)S(1)}, u32[]{:S(2)}, u32[]{:S(2)}) collective-permute-start(f32[49,128]{1,0:T(8,128)S(1)} %collective-permute-done.2), channel_id=1, source_target_pairs={{0,12},{4,0},{8,4},{12,8},{1,13},{5,1},{9,5},{13,9},{2,14},{6,2},{... | collective-permute-start | bytes 75272 | tf_op jit(solution)/shard_map/ppermute | solution.py:85
  81.8 3.9 %collective-permute-start.4 = (f32[49,128]{1,0:T(8,128)S(1)}, f32[49,128]{1,0:T(8,128)S(1)}, u32[]{:S(2)}, u32[]{:S(2)}) collective-permute-start(f32[49,128]{1,0:T(8,128)S(1)} %collective-permute-done.3), channel_id=1, source_target_pairs={{0,12},{4,0},{8,4},{12,8},{1,13},{5,1},{9,5},{13,9},{2,14},{6,2},{... | collective-permute-start | bytes 75272 | tf_op jit(solution)/shard_map/ppermute | solution.py:85
  86.8 1.3 %copy-start.7 = (f32[32,65,128]{2,1,0:T(8,128)S(1)}, f32[32,65,128]{2,1,0:T(8,128)}, u32[]{:S(2)}) copy-start(f32[32,65,128]{2,1,0:T(8,128)} %pad_maximum_fusion.3) | copy-start | bytes 3194884
  86.8 1.6 %copy-start.8 = (f32[32,64,128]{2,1,0:T(8,128)S(1)}, f32[32,64,128]{2,1,0:T(8,128)}, u32[]{:S(2)}) copy-start(f32[32,64,128]{2,1,0:T(8,128)} %pad_maximum_fusion.6) | copy-start | bytes 3145732
  88.4 1.6 %copy-start.4 = (f32[2,16,64,129]{3,2,1,0:T(8,128)S(1)}, f32[2,16,64,129]{3,2,1,0:T(8,128)}, u32[]{:S(2)}) copy-start(f32[2,16,64,129]{3,2,1,0:T(8,128)} %subtract_multiply_fusion) | copy-start | bytes 3170308
  88.4 1.7 %copy-start.6 = (f32[16,64,128]{2,1,0:T(8,128)S(1)}, f32[16,64,128]{2,1,0:T(8,128)}, u32[]{:S(2)}) copy-start(f32[16,64,128]{2,1,0:T(8,128)} %copy-done.5) | copy-start | bytes 1572868
  88.4 2.0 %copy-start.9 = (f32[2,15,64,128]{3,2,1,0:T(8,128)S(1)}, f32[2,15,64,128]{3,2,1,0:T(8,128)}, u32[]{:S(2)}) copy-start(f32[2,15,64,128]{3,2,1,0:T(8,128)} %fusion.7) | copy-start | bytes 2949124
